TPU v7x, 32 devices: a whole 2x2x4 slice. The times are simulated.
32 devices in a mesh: freq: 4 (over y, x), band: 8 (over z, core).
Axes of the slice: x: 2, y: 2, z: 4, core: 2. Of those that a mesh axis runs over, the one named last changes fastest.
Arguments:
- pair_density: bfloat16 [1024, 2, 8192], P(('freq', 'band')), may hold values from -6 to 6
- trial_vectors: bfloat16 [16, 2, 64, 8192], P('freq', None, None, 'band'), may hold values from -6 to 6
- frequency: float32 [16], P('freq'), may hold values from 0.05 to 20
- val_energy: float32 [32], replicated, may hold values from -3 to -0.1
- cond_energy: float32 [32], replicated, may hold values from 0.1 to 4
- pair_index: int32 [1024], P(('freq', 'band')), may hold values from 0 to 1023, each once
Outputs:
- images: float32 [16, 2, 64, 8192], P('freq', None, None, 'band')
- subspace: float32 [16, 2, 64, 64], P('freq')
Inputs may be any that keep to these rules, and one draw needn't show every extreme that they name: `pair_index`: every pair number 0 to 1023 appears exactly once.
All inputs are finite; a program needn't handle non-finite values.
Results may differ from a plain program's by a relative error of at most 0.0085.
Values may be sent and summed in bfloat16 or wider, within the bound.
No kernel may reach another device: no remote copies, remote signals or barrier semaphores. Data moves between devices by JAX's collectives and lax.ppermute only.
A program may use at most 128 MiB of HBM per device.

v0:
```python
import math
import jax
import jax.numpy as jnp
from jax import lax
from jax.sharding import PartitionSpec as P


def local_weights(pair_index, frequency, val_energy, cond_energy, prefactor):
    cond_count = cond_energy.shape[0]
    val_count = val_energy.shape[0]
    cond_pick = jnp.sum(
        jnp.where(
            (pair_index % cond_count)[:, None] == jnp.arange(cond_count)[None, :],
            cond_energy[None, :],
            0.0,
        ),
        axis=1,
    )
    val_pick = jnp.sum(
        jnp.where(
            (pair_index // cond_count)[:, None] == jnp.arange(val_count)[None, :],
            val_energy[None, :],
            0.0,
        ),
        axis=1,
    )
    delta = cond_pick - val_pick
    ratio = delta[:, None] / (
        delta[:, None] * delta[:, None] + frequency[None, :] * frequency[None, :]
    )
    return (-4.0 * prefactor * ratio).astype(jnp.bfloat16)


def crossing_terms(density, vectors):
    products = jnp.einsum("pcg,fekg->fcekp", density, vectors, preferred_element_type=jnp.float32)
    return jnp.stack(
        [products[:, 0, 0] + products[:, 1, 1], products[:, 0, 1] - products[:, 1, 0]], 1
    )


def scale_terms(crossings, weights):
    factor = jnp.transpose(weights.astype(jnp.float32))[:, None, None, :]
    return (factor * crossings).astype(jnp.bfloat16)


def mix_terms(scaled):
    scaled_real = scaled[:, 0]
    scaled_imag = scaled[:, 1]
    return jnp.stack(
        [jnp.stack([scaled_real, -scaled_imag], 1), jnp.stack([scaled_imag, scaled_real], 1)], 1
    )


def image_terms(density, mixed):
    return jnp.einsum("pcg,fdckp->fdkg", density, mixed, preferred_element_type=jnp.float32)


def shards(pair_density, trial_vectors, frequency, val_energy, cond_energy, pair_index):
    groups = lax.axis_size("freq")
    members = lax.axis_size("band")
    pair_count = pair_density.shape[0] * groups * members
    grid_count = trial_vectors.shape[3] * members
    prefactor = 1.0 / math.sqrt(2.0 * grid_count * pair_count)
    regrouped = lax.all_to_all(pair_density, "band", split_axis=2, concat_axis=0, tiled=True)
    grouped = lax.all_gather(regrouped, "freq", axis=0, tiled=True)
    all_index = lax.all_gather(pair_index, ("freq", "band"), axis=0, tiled=True)
    crossings = crossing_terms(grouped, trial_vectors)
    summed = lax.psum(crossings, "band")
    all_weights = local_weights(all_index, frequency, val_energy, cond_energy, prefactor)
    scaled = scale_terms(summed, all_weights)
    images = image_terms(grouped, mix_terms(scaled))
    vectors = trial_vectors.astype(jnp.float32)
    highest = lax.Precision.HIGHEST
    real_part = jnp.einsum(
        "fkg,flg->fkl", vectors[:, 0], images[:, 0], precision=highest
    ) + jnp.einsum("fkg,flg->fkl", vectors[:, 1], images[:, 1], precision=highest)
    imag_part = jnp.einsum(
        "fkg,flg->fkl", vectors[:, 0], images[:, 1], precision=highest
    ) - jnp.einsum("fkg,flg->fkl", vectors[:, 1], images[:, 0], precision=highest)
    partial_value = jnp.stack([real_part, imag_part], 1) / grid_count
    subspace = lax.psum(partial_value, "band")
    return (images, subspace)


def solution(mesh):
    return jax.shard_map(
        shards,
        mesh=mesh,
        in_specs=(
            P(("freq", "band"), None, None),
            P("freq", None, None, "band"),
            P("freq"),
            P(),
            P(),
            P(("freq", "band")),
        ),
        out_specs=(P("freq", None, None, "band"), P("freq", None, None, None)),
        check_vma=False,
    )
```

profile of v0, /device:TPU:0, one launch (start us, length us, event | category | flops | bytes accessed | tf_op | source)
XLA Modules:
  0.0 269.7 jit_solution(9058504637230988360)
XLA Ops:
  7.2 10.8 %copy.31 = bf16[32,2,8192]{0,1,2:T(2,128)(2,1)} copy(bf16[32,2,8192]{2,1,0:T(2,128)(2,1)} %param.6) | data formatting | bytes 2097152 | tf_op args[0]
  18.0 7.0 %reshape.101 = bf16[8,2,32768]{2,1,0:T(2,128)(2,1)S(1)} reshape(bf16[8192,2,32]{2,1,0:T(2,128)(2,1)} %bitcast.76) | data formatting | bytes 2097152
  24.9 32.7 %all_to_all.18 = bf16[8,2,32768]{2,1,0:T(2,128)(2,1)S(1)} all-to-all(bf16[8,2,32768]{2,1,0:T(2,128)(2,1)S(1)} %reshape.101), channel_id=1, replica_groups=mesh['freq'=4,'band'=8] {'band'}, dimensions={0} | all-to-all | bytes 2097152 | tf_op jit(solution)/shard_map/all_to_all | solution.py:64
  57.7 4.5 %reshape.102 = bf16[8192,2,32]{2,1,0:T(2,128)(2,1)} reshape(bf16[8,2,32768]{2,1,0:T(2,128)(2,1)S(1)} %all_to_all.18) | data formatting | bytes 2097152
  62.2 10.5 %copy.32 = bf16[32,2,8,1024]{3,0,2,1:T(8,128)(2,1)} copy(bf16[32,2,8,1024]{0,1,3,2:T(2,128)(2,1)} %bitcast.75) | data formatting | bytes 2097152 | tf_op jit(solution)/shard_map/all_to_all | solution.py:64
  72.7 51.6 %all-gather.2.cloned.1.call-done = bf16[1024,2,1024]{2,0,1:T(8,128)(2,1)} async-done(((bf16[256,2,1024]{2,0,1:T(8,128)(2,1)}), bf16[1024,2,1024]{2,0,1:T(8,128)(2,1)}) %all-gather.2.cloned.1.call-update) | async-done | bytes 4194320 | tf_op jit(solution)/shard_map/all_gather | solution.py:65
  124.3 4.6 %fusion.4 = f32[4,2,2,64,1024]{4,3,1,2,0:T(8,128)S(1)} fusion(bf16[1024,2,1024]{2,0,1:T(8,128)(2,1)} %all-gather.2.cloned.1.call-done, bf16[4,2,64,1024]{3,2,1,0:T(8,128)(2,1)S(1)} %copy-done.1), kind=kOutput, calls=%fused_computation.4 | convolution fusion | flops 2147483648 | bytes 9437184 | tf_op jit(solution)/shard_map/pcg,fekg->fcekp/dot_general | solution.py:35
  128.9 0.1 fusion.15
  129.2 1.5 pad_maximum_fusion
  130.7 0.6 copy-done.5
  131.3 0.2 dynamic-update-slice
  131.5 39.6 %all-reduce = s32[1024]{0:T(1024)S(1)} all-reduce(s32[1024]{0:T(1024)S(1)} %dynamic-update-slice), channel_id=1, replica_groups=mesh['freq'=4,'band'=8] {'freq','band'}, use_global_device_ids=true, to_apply=%add | all-reduce | flops 1024 | bytes 8192
  171.4 25.1 %all-reduce.4.cloned.1.call-done = f32[4,2,64,1024]{3,2,0,1:T(8,128)} async-done(((f32[4,2,64,1024]{3,2,0,1:T(8,128)}), f32[4,2,64,1024]{3,2,0,1:T(8,128)}) %all-reduce.4.cloned.1.call-update) | async-done | bytes 2097168 | tf_op jit(solution)/shard_map/psum | solution.py:68
  196.5 1.8 multiply_convert_fusion
  198.5 0.2 maximum_bitcast_fusion
  198.7 1.9 copy-done.4
  200.5 2.3 fusion.8
  202.9 0.6 fusion.20
  203.5 0.6 fusion.19
  204.2 0.6 fusion.13
  204.8 0.6 fusion.14
  205.4 0.7 maximum_multiply_fusion
  206.2 55.2 %all-reduce.6.cloned.1.call-done = f32[4,2,64,64]{2,3,0,1:T(8,128)} async-done(((f32[4,2,64,64]{2,3,0,1:T(8,128)}), f32[4,2,64,64]{2,3,0,1:T(8,128)}) %all-reduce.6.cloned.1.call-update) | async-done | bytes 131088 | tf_op jit(solution)/shard_map/psum | solution.py:81
  261.4 1.8 copy.38
  (26 shorter events, 0.7 us)
Async XLA Ops:
  7.2 117.1 %all-gather.2.cloned.1.call-start = ((), (), s32[]{:S(2)}) async-start(), calls=%async_computation.1 | async-start | bytes 5242880 | tf_op jit(solution)/shard_map/all_gather | solution.py:65
  62.2 62.2 %copy-start.1 = (bf16[4,2,64,1024]{3,2,1,0:T(8,128)(2,1)S(1)}, bf16[4,2,64,1024]{3,2,1,0:T(8,128)(2,1)}, u32[]{:S(2)}) copy-start(bf16[4,2,64,1024]{3,2,1,0:T(8,128)(2,1)} %param.7) | copy-start | bytes 3145732
  72.6 123.9 %all-reduce.4.cloned.1.call-start = ((), (), s32[]{:S(2)}) async-start(), calls=%async_computation.2 | async-start | bytes 4194304 | tf_op jit(solution)/shard_map/psum | solution.py:68
  130.6 0.7 copy-start.5
  130.6 0.7 copy-start.6
  130.6 40.6 %copy-start.2 = (f32[32]{0:T(128)S(1)}, f32[32]{0:T(128)}, u32[]{:S(2)}) copy-start(f32[32]{0:T(128)} %param.9) | copy-start | bytes 388
  130.6 40.6 %copy-start.3 = (f32[32]{0:T(128)S(1)}, f32[32]{0:T(128)}, u32[]{:S(2)}) copy-start(f32[32]{0:T(128)} %param.10) | copy-start | bytes 388
  130.7 130.8 %all-reduce.6.cloned.1.call-start = ((), (), s32[]{:S(2)}) async-start(), calls=%async_computation.3 | async-start | bytes 524288 | tf_op jit(solution)/shard_map/psum | solution.py:81
  198.4 2.2 copy-start.4
  202.9 1.9 copy-start
Sparse Core Ops, SparseCore 0:
  72.8 51.4 all-gather.1
  130.8 65.6 all-reduce.3
  206.3 55.0 all-reduce.5
where the time goes:
time: 271 us; the launch traced here: 270 us
  waiting for transfers between devices  132 us (49%)
  blocking collectives  72.4 us (27%)
  local copies, waits for them, and re-layouts  37.2 us (14%)
  between operations  13.9 us (5%)
  matrix products  9.4 us (3%)
  other arithmetic  4.8 us (2%)
    psum x1, waiting for transfers between devices, shards(): subspace = lax.psum(partial_value, 'band')  55.2 us
    all_gather x1, waiting for transfers between devices, shards(): grouped = lax.all_gather(regrouped, 'freq', axis=0, tiled=True)  51.6 us
    unnamed x1, blocking collectives  39.6 us
    all_to_all x1, blocking collectives, shards(): lax.all_to_all(pair_density, 'band', split_axis=2, concat_axis=0, tiled=T...  32.7 us
    unnamed x20, local copies, waits for them, and re-layouts  26.7 us
    psum x1, waiting for transfers between devices, shards(): summed = lax.psum(crossings, 'band')  25.1 us
    all_to_all x1, local copies, waits for them, and re-layouts, shards(): lax.all_to_all(pair_density, 'band', split_axis=2, concat_axis=0, tiled=T...  10.5 us
  transfers between devices with their start and end apart: 3, of which 3 were waited for; matrix products, arithmetic and copies ran while one was open for 0% of the time, Pallas kernels for 0%

commit v1 on v0

--- a/solution.py
+++ b/solution.py
@@ -61,7 +61,9 @@
     pair_count = pair_density.shape[0] * groups * members
     grid_count = trial_vectors.shape[3] * members
     prefactor = 1.0 / math.sqrt(2.0 * grid_count * pair_count)
-    regrouped = lax.all_to_all(pair_density, "band", split_axis=2, concat_axis=0, tiled=True)
+    cells = jnp.split(pair_density, lax.axis_size("band"), axis=2)
+    arrived = lax.all_to_all(jnp.stack(cells), "band", 0, 0)
+    regrouped = jnp.concatenate(arrived, axis=0)
     grouped = lax.all_gather(regrouped, "freq", axis=0, tiled=True)
     all_index = lax.all_gather(pair_index, ("freq", "band"), axis=0, tiled=True)
     crossings = crossing_terms(grouped, trial_vectors)

time: 271 us -> 247 us (0.911)
  local copies, waits for them, and re-layouts: 37.2 us -> 13.8 us
    unnamed x20 -> x24, local copies, waits for them, and re-layouts: 26.7 us -> 11.6 us
    all_to_all x1, local copies, waits for them, and re-layouts: 10.5 us -> 1.25 us  [shards(): arrived = lax.all_to_all(jnp.stack(cells), 'band', 0, 0)]
where the time goes in v1:
time: 247 us
  waiting for transfers between devices  132 us (53%)
  blocking collectives  72.4 us (29%)
  between operations  13.9 us (6%)
  local copies, waits for them, and re-layouts  13.8 us (6%)
  matrix products  9.4 us (4%)
  other arithmetic  4.91 us (2%)
    psum x1, waiting for transfers between devices, shards(): subspace = lax.psum(partial_value, 'band')  55.2 us
    all_gather x1, waiting for transfers between devices, shards(): grouped = lax.all_gather(regrouped, 'freq', axis=0, tiled=True)  51.6 us
    unnamed x1, blocking collectives  39.6 us
    all_to_all x1, blocking collectives, shards(): arrived = lax.all_to_all(jnp.stack(cells), 'band', 0, 0)  32.7 us
    psum x1, waiting for transfers between devices, shards(): summed = lax.psum(crossings, 'band')  25.1 us
    unnamed x24, local copies, waits for them, and re-layouts  11.6 us
  transfers between devices with their start and end apart: 3, of which 3 were waited for; matrix products, arithmetic and copies ran while one was open for 0% of the time, Pallas kernels for 0%

profile of v1, /device:TPU:0, one launch (start us, length us, event | category | flops | bytes accessed | tf_op | source)
XLA Modules:
  0.0 246.5 jit_solution(2430290449364862297)
XLA Ops:
  7.2 1.0 bitcast_dynamic-update-slice_fusion.7
  8.2 1.0 bitcast_dynamic-update-slice_fusion.6
  9.2 1.0 bitcast_dynamic-update-slice_fusion.5
  10.2 1.0 bitcast_dynamic-update-slice_fusion.4
  11.3 1.0 bitcast_dynamic-update-slice_fusion.3
  12.3 1.0 bitcast_dynamic-update-slice_fusion.2
  13.3 1.0 bitcast_dynamic-update-slice_fusion.1
  14.3 1.0 bitcast_dynamic-update-slice_fusion
  15.3 32.7 %all_to_all.5 = bf16[8,32,2,1024]{3,2,1,0:T(2,128)(2,1)S(1)} all-to-all(bf16[8,32,2,1024]{3,2,1,0:T(2,128)(2,1)S(1)} %bitcast_dynamic-update-slice_fusion), channel_id=1, replica_groups=mesh['freq'=4,'band'=8] {'band'}, dimensions={0} | all-to-all | bytes 2097152 | tf_op jit(solution)/shard_map/all_to_all | solution.py:65
  48.0 1.3 copy.15
  49.4 51.6 %all-gather.2.cloned.1.call-done = bf16[1024,2,1024]{2,0,1:T(8,128)(2,1)} async-done(((bf16[256,2,1024]{2,0,1:T(8,128)(2,1)}), bf16[1024,2,1024]{2,0,1:T(8,128)(2,1)}) %all-gather.2.cloned.1.call-update) | async-done | bytes 4194320 | tf_op jit(solution)/shard_map/all_gather | solution.py:67
  101.0 4.6 %fusion.4 = f32[4,2,2,64,1024]{4,3,2,0,1:T(8,128)S(1)} fusion(bf16[1024,2,1024]{2,0,1:T(8,128)(2,1)} %all-gather.2.cloned.1.call-done, bf16[4,2,64,1024]{3,2,1,0:T(8,128)(2,1)S(1)} %copy-done.1), kind=kOutput, calls=%fused_computation.4 | convolution fusion | flops 2147483648 | bytes 9437184 | tf_op jit(solution)/shard_map/pcg,fekg->fcekp/dot_general | solution.py:35
  105.9 1.5 pad_maximum_fusion
  108.3 39.6 %all-reduce = s32[1024]{0:T(1024)S(1)} all-reduce(s32[1024]{0:T(1024)S(1)} %dynamic-update-slice), channel_id=1, replica_groups=mesh['freq'=4,'band'=8] {'freq','band'}, use_global_device_ids=true, to_apply=%add | all-reduce | flops 1024 | bytes 8192
  148.2 25.1 %all-reduce.4.cloned.1.call-done = f32[4,2,64,1024]{3,2,0,1:T(8,128)} async-done(((f32[4,2,64,1024]{3,2,0,1:T(8,128)}), f32[4,2,64,1024]{3,2,0,1:T(8,128)}) %all-reduce.4.cloned.1.call-update) | async-done | bytes 2097168 | tf_op jit(solution)/shard_map/psum | solution.py:70
  173.3 1.8 multiply_convert_fusion
  175.4 1.9 copy-done.4
  177.3 2.3 fusion.8
  179.7 0.6 fusion.20
  180.9 0.6 fusion.13
  181.6 0.6 fusion.14
  182.2 0.7 maximum_multiply_fusion
  183.0 55.2 %all-reduce.6.cloned.1.call-done = f32[4,2,64,64]{2,3,0,1:T(8,128)} async-done(((f32[4,2,64,64]{2,3,0,1:T(8,128)}), f32[4,2,64,64]{2,3,0,1:T(8,128)}) %all-reduce.6.cloned.1.call-update) | async-done | bytes 131088 | tf_op jit(solution)/shard_map/psum | solution.py:83
  238.2 1.8 copy.21
  (31 shorter events, 2.4 us)
Async XLA Ops:
  7.2 93.8 %all-gather.2.cloned.1.call-start = ((), (), s32[]{:S(2)}) async-start(), calls=%async_computation.1 | async-start | bytes 5242880 | tf_op jit(solution)/shard_map/all_gather | solution.py:67
  48.0 52.9 %copy-start.1 = (bf16[4,2,64,1024]{3,2,1,0:T(8,128)(2,1)S(1)}, bf16[4,2,64,1024]{3,2,1,0:T(8,128)(2,1)}, u32[]{:S(2)}) copy-start(bf16[4,2,64,1024]{3,2,1,0:T(8,128)(2,1)} %param.7) | copy-start | bytes 3145732
  49.3 124.0 %all-reduce.4.cloned.1.call-start = ((), (), s32[]{:S(2)}) async-start(), calls=%async_computation.2 | async-start | bytes 4194304 | tf_op jit(solution)/shard_map/psum | solution.py:70
  107.4 0.7 copy-start.5
  107.4 0.7 copy-start.6
  107.4 40.6 %copy-start.2 = (f32[32]{0:T(128)S(1)}, f32[32]{0:T(128)}, u32[]{:S(2)}) copy-start(f32[32]{0:T(128)} %param.9) | copy-start | bytes 388
  107.4 40.6 %copy-start.3 = (f32[32]{0:T(128)S(1)}, f32[32]{0:T(128)}, u32[]{:S(2)}) copy-start(f32[32]{0:T(128)} %param.10) | copy-start | bytes 388
  107.4 130.8 %all-reduce.6.cloned.1.call-start = ((), (), s32[]{:S(2)}) async-start(), calls=%async_computation.3 | async-start | bytes 524288 | tf_op jit(solution)/shard_map/psum | solution.py:83
  175.1 2.2 copy-start.4
  179.7 1.9 copy-start
Sparse Core Ops, SparseCore 0:
  49.4 51.4 all-gather.1
  107.5 65.6 all-reduce.3
  183.1 55.0 all-reduce.5

commit v2 on v0

--- a/solution.py
+++ b/solution.py
@@ -78,7 +78,8 @@
         "fkg,flg->fkl", vectors[:, 0], images[:, 1], precision=highest
     ) - jnp.einsum("fkg,flg->fkl", vectors[:, 1], images[:, 0], precision=highest)
     partial_value = jnp.stack([real_part, imag_part], 1) / grid_count
-    subspace = lax.psum(partial_value, "band")
+    parts = lax.all_gather(partial_value, "band", axis=0, tiled=False)
+    subspace = parts.sum(axis=0)
     return (images, subspace)
 
 

time: 271 us -> 246 us (0.908)
  waiting for transfers between devices: 132 us -> 106 us
    psum x1 -> x0, waiting for transfers between devices: 55.2 us -> none  [shards(): subspace = lax.psum(partial_value, 'band')]
    all_gather x0 -> x1, waiting for transfers between devices: none -> 28.9 us  [shards(): parts = lax.all_gather(partial_value, 'band', axis=0, tiled=False)]
    unnamed x20 -> x19, local copies, waits for them, and re-layouts: 26.7 us -> 24.9 us
where the time goes in v2:
time: 246 us; the launch traced here: 244 us
  waiting for transfers between devices  106 us (43%)
  blocking collectives  72.3 us (29%)
  local copies, waits for them, and re-layouts  36.2 us (15%)
  between operations  13.9 us (6%)
  matrix products  9.4 us (4%)
  other arithmetic  6.63 us (3%)
    all_gather x1, waiting for transfers between devices, shards(): grouped = lax.all_gather(regrouped, 'freq', axis=0, tiled=True)  51.6 us
    unnamed x1, blocking collectives  39.6 us
    all_to_all x1, blocking collectives, shards(): lax.all_to_all(pair_density, 'band', split_axis=2, concat_axis=0, tiled=T...  32.7 us
    all_gather x1, waiting for transfers between devices, shards(): parts = lax.all_gather(partial_value, 'band', axis=0, tiled=False)  28.9 us
    psum x1, waiting for transfers between devices, shards(): summed = lax.psum(crossings, 'band')  25.2 us
    unnamed x19, local copies, waits for them, and re-layouts  24.9 us
    all_to_all x1, local copies, waits for them, and re-layouts, shards(): lax.all_to_all(pair_density, 'band', split_axis=2, concat_axis=0, tiled=T...  10.5 us
  transfers between devices with their start and end apart: 3, of which 3 were waited for; matrix products, arithmetic and copies ran while one was open for 0% of the time, Pallas kernels for 0%

profile of v2, /device:TPU:0, one launch (start us, length us, event | category | flops | bytes accessed | tf_op | source)
XLA Modules:
  0.0 244.3 jit_solution(1319014893914900127)
XLA Ops:
  7.2 10.8 %copy.34 = bf16[32,2,8192]{0,1,2:T(2,128)(2,1)} copy(bf16[32,2,8192]{2,1,0:T(2,128)(2,1)} %param.6) | data formatting | bytes 2097152 | tf_op args[0]
  18.0 7.0 %reshape.132 = bf16[8,2,32768]{2,1,0:T(2,128)(2,1)S(1)} reshape(bf16[8192,2,32]{2,1,0:T(2,128)(2,1)} %bitcast.76) | data formatting | bytes 2097152
  25.0 32.7 %all_to_all.18 = bf16[8,2,32768]{2,1,0:T(2,128)(2,1)S(1)} all-to-all(bf16[8,2,32768]{2,1,0:T(2,128)(2,1)S(1)} %reshape.132), channel_id=1, replica_groups=mesh['freq'=4,'band'=8] {'band'}, dimensions={0} | all-to-all | bytes 2097152 | tf_op jit(solution)/shard_map/all_to_all | solution.py:64
  57.7 4.5 %reshape.133 = bf16[8192,2,32]{2,1,0:T(2,128)(2,1)} reshape(bf16[8,2,32768]{2,1,0:T(2,128)(2,1)S(1)} %all_to_all.18) | data formatting | bytes 2097152
  62.2 10.5 %copy.35 = bf16[32,2,8,1024]{3,0,2,1:T(8,128)(2,1)} copy(bf16[32,2,8,1024]{0,1,3,2:T(2,128)(2,1)} %bitcast.75) | data formatting | bytes 2097152 | tf_op jit(solution)/shard_map/all_to_all | solution.py:64
  72.7 51.6 %all-gather.3.cloned.1.call-done = bf16[1024,2,1024]{2,0,1:T(8,128)(2,1)} async-done(((bf16[256,2,1024]{2,0,1:T(8,128)(2,1)}), bf16[1024,2,1024]{2,0,1:T(8,128)(2,1)}) %all-gather.3.cloned.1.call-update) | async-done | bytes 4194320 | tf_op jit(solution)/shard_map/all_gather | solution.py:65
  124.3 4.6 %fusion.4 = f32[4,2,2,64,1024]{4,3,1,2,0:T(8,128)S(1)} fusion(bf16[1024,2,1024]{2,0,1:T(8,128)(2,1)} %all-gather.3.cloned.1.call-done, bf16[4,2,64,1024]{3,2,1,0:T(8,128)(2,1)S(1)} %copy-done.1), kind=kOutput, calls=%fused_computation.4 | convolution fusion | flops 2147483648 | bytes 9437184 | tf_op jit(solution)/shard_map/pcg,fekg->fcekp/dot_general | solution.py:35
  128.9 0.1 fusion.15
  129.2 1.5 pad_maximum_fusion
  130.7 0.6 copy-done.5
  131.3 0.2 dynamic-update-slice
  131.5 39.6 %all-reduce = s32[1024]{0:T(1024)S(1)} all-reduce(s32[1024]{0:T(1024)S(1)} %dynamic-update-slice), channel_id=1, replica_groups=mesh['freq'=4,'band'=8] {'freq','band'}, use_global_device_ids=true, to_apply=%add | all-reduce | flops 1024 | bytes 8192
  171.4 25.2 %all-reduce.3.cloned.1.call-done = f32[4,2,64,1024]{3,2,0,1:T(8,128)} async-done(((f32[4,2,64,1024]{3,2,0,1:T(8,128)}), f32[4,2,64,1024]{3,2,0,1:T(8,128)}) %all-reduce.3.cloned.1.call-update) | async-done | bytes 2097168 | tf_op jit(solution)/shard_map/psum | solution.py:68
  196.5 1.8 multiply_convert_fusion
  198.5 0.2 maximum_bitcast_fusion
  198.7 1.9 copy-done.4
  200.6 2.3 fusion.8
  202.9 0.6 fusion.20
  203.6 0.6 fusion.19
  204.2 0.6 fusion.13
  204.8 0.6 fusion.14
  205.5 0.8 copy.41
  206.4 28.9 %all-gather.5.cloned.1.call-done = f32[8,4,2,64,64]{4,3,2,1,0:T(8,128)} async-done(((f32[1,4,2,64,64]{4,3,2,1,0:T(8,128)}), f32[8,4,2,64,64]{4,3,2,1,0:T(8,128)}) %all-gather.5.cloned.1.call-update) | async-done | bytes 1048592 | tf_op jit(solution)/shard_map/all_gather | solution.py:81
  235.3 2.5 %reduce_sum.29 = f32[4,2,64,64]{3,2,1,0:T(8,128)} reduce(f32[8,4,2,64,64]{4,3,2,1,0:T(8,128)} %all-gather.5.cloned.1.call-done, f32[]{:T(128)} %constant.29.clone.1), dimensions={0}, to_apply=%region_3.4 | reduce | flops 229376 | bytes 1179652 | tf_op jit(solution)/shard_map/reduce_sum | solution.py:82
  (27 shorter events, 0.7 us)
Async XLA Ops:
  7.2 117.1 %all-gather.3.cloned.1.call-start = ((), (), s32[]{:S(2)}) async-start(), calls=%async_computation.1 | async-start | bytes 5242880 | tf_op jit(solution)/shard_map/all_gather | solution.py:65
  62.2 62.2 %copy-start.1 = (bf16[4,2,64,1024]{3,2,1,0:T(8,128)(2,1)S(1)}, bf16[4,2,64,1024]{3,2,1,0:T(8,128)(2,1)}, u32[]{:S(2)}) copy-start(bf16[4,2,64,1024]{3,2,1,0:T(8,128)(2,1)} %param.7) | copy-start | bytes 3145732
  72.6 123.9 %all-reduce.3.cloned.1.call-start = ((), (), s32[]{:S(2)}) async-start(), calls=%async_computation.2 | async-start | bytes 4194304 | tf_op jit(solution)/shard_map/psum | solution.py:68
  130.6 0.7 copy-start.5
  130.6 0.7 copy-start.6
  130.6 40.5 %copy-start.2 = (f32[32]{0:T(128)S(1)}, f32[32]{0:T(128)}, u32[]{:S(2)}) copy-start(f32[32]{0:T(128)} %param.9) | copy-start | bytes 388
  130.6 40.5 %copy-start.3 = (f32[32]{0:T(128)S(1)}, f32[32]{0:T(128)}, u32[]{:S(2)}) copy-start(f32[32]{0:T(128)} %param.10) | copy-start | bytes 388
  130.7 104.6 %all-gather.5.cloned.1.call-start = ((), (), s32[]{:S(2)}) async-start(), calls=%async_computation.3 | async-start | bytes 2359296 | tf_op jit(solution)/shard_map/all_gather | solution.py:81
  198.4 2.2 copy-start.4
  202.9 1.9 copy-start
Sparse Core Ops, SparseCore 0:
  72.8 51.4 all-gather.2
  130.8 65.7 all-reduce.2
  206.5 28.7 all-gather.4
